TPU v7x, 128 devices: a whole 4x4x4 slice. The times are simulated.
128 devices in a mesh: seq: 64 (over z, y, x), tp: 2 (over core).
Axes of the slice: x: 4, y: 4, z: 4, core: 2. Of those that a mesh axis runs over, the one named last changes fastest.
Arguments:
- patches: bfloat16 [16384, 1280], P('seq'), may hold values from -60 to 60
- merge_up: bfloat16 [5120, 2560], P(None, 'tp'), may hold values from -0.078125 to 0.078125
- merge_down: bfloat16 [2560, 3584], P('tp'), may hold values from -0.125 to 0.125
- dest: int32 [4096], P('seq'), may hold values from 0 to 63, as said below
- slot: int32 [4096], P('seq'), may hold values from 0 to 255, as said below
- text: bfloat16 [16384, 3584], P('seq'), may hold values from -60 to 60
- positions: int32 [3, 16384], P(None, 'seq'), may hold values from 0 to 1023
- documents: int32 [16384], P('seq'), may hold values from 0 to 7, never falling along the last dimension, each value on 1 to 8448 neighbouring positions
- w_query: bfloat16 [3584, 1792], P('seq', 'tp'), may hold values from -8 to 8
- w_key: bfloat16 [3584, 256], P('seq', 'tp'), may hold values from -8 to 8
- w_value: bfloat16 [3584, 256], P('seq', 'tp'), may hold values from -0.09375 to 0.09375
Outputs:
- layer_input: bfloat16 [16384, 3584], P('seq', 'tp')
- attended: bfloat16 [16384, 1792], P('seq', 'tp')
Inputs may be any that keep to these rules, and one draw needn't show every extreme that they name: `dest`: the rows of one device name each sequence shard at most 2 times, and in every draw some sequence shard is named 2 times by the rows of every device. `slot`: no two image rows share both a sequence shard and a position. `documents`: document numbers never fall along the tokens.
All inputs are finite; a program needn't handle non-finite values.
Results may differ from a plain program's by a relative error of at most 0.0065.
Values may be sent and summed in bfloat16 or wider, within the bound.
A program may use at most 128 MiB of HBM per device.

v0:
```python
import jax
import jax.numpy as jnp
from jax import lax
from jax.sharding import PartitionSpec as P

HEAD = 128
epsilon = 1e-06
theta_base = 1000000.0
masked_score = -1e30
block_rows = 512


def copy_for_each(x, axis):
    size = lax.axis_size(axis)
    return lax.all_to_all(jnp.broadcast_to(x[None], (size, *x.shape)), axis, 0, 0, tiled=True)


def of_everyone(x, axis):
    everything = copy_for_each(x, axis)
    return jnp.sum(everything, axis=0)


def sent_together(arrays, axis, dim, along):
    ends, at = ([], 0)
    for a in arrays[:-1]:
        at += a.shape[along]
        ends.append(at)
    both = jnp.concatenate(arrays, axis=along)
    return tuple(jnp.split(lax.all_gather(both, axis, axis=dim, tiled=True), ends, axis=along))


def rms_rows(values):
    floats = values.astype(jnp.float32)
    return floats * lax.rsqrt(jnp.mean(floats * floats, axis=-1, keepdims=True) + epsilon)


def rotate(vectors, positions):
    half_dim = vectors.shape[-1] // 2
    first_end = half_dim // 4
    second_end = first_end + 3 * half_dim // 8
    pair_ids = jnp.arange(half_dim, dtype=jnp.int32)
    inverse = jnp.power(theta_base, -2.0 * pair_ids.astype(jnp.float32) / (2 * half_dim))
    coords = positions.astype(jnp.float32)
    chosen = jnp.where(
        pair_ids[None, :] < first_end,
        coords[0][:, None],
        jnp.where(pair_ids[None, :] < second_end, coords[1][:, None], coords[2][:, None]),
    )
    angles = chosen * inverse[None, :]
    cosine = jnp.cos(angles)[:, None, :]
    sine = jnp.sin(angles)[:, None, :]
    lower_part = vectors[..., :half_dim]
    upper_part = vectors[..., half_dim:]
    return jnp.concatenate(
        [lower_part * cosine - upper_part * sine, upper_part * cosine + lower_part * sine], axis=-1
    )


def attend(
    carry, queries, key_block, value_block, doc_block, key_first, query_pos, query_doc, score_scale
):
    maxima, totals, summed = carry
    scores = (
        jnp.einsum("qkgd,pkd->kgqp", queries, key_block, preferred_element_type=jnp.float32)
        * score_scale
    )
    key_pos = key_first + jnp.arange(key_block.shape[0], dtype=jnp.int32)
    allowed = (query_pos[:, None] >= key_pos[None, :]) & (query_doc[:, None] == doc_block[None, :])
    scores = jnp.where(allowed, scores, masked_score)
    new_max = jnp.maximum(maxima, jnp.max(scores, axis=-1))
    weights = jnp.where(allowed, jnp.exp(scores - new_max[..., None]), 0.0)
    factor = jnp.exp(maxima - new_max)
    totals = totals * factor + jnp.sum(weights, axis=-1)
    summed = summed * factor[..., None] + jnp.einsum(
        "kgqp,pkd->kgqd",
        weights.astype(jnp.bfloat16),
        value_block,
        preferred_element_type=jnp.float32,
    )
    return (new_max, totals, summed)


def per_device(
    patches, merge_up, merge_down, dest, slot, text, positions, documents, w_query, w_key, w_value
):
    seq_count = lax.axis_size("seq")
    tp_count = lax.axis_size("tp")
    tok_dev = text.shape[0]
    model_width = text.shape[1]
    img_dev = dest.shape[0]
    capacity = max(2, 2 * img_dev // seq_count)
    grouped = rms_rows(patches).astype(jnp.bfloat16).reshape(img_dev, -1)
    merger_hidden = jax.nn.gelu(
        jnp.dot(grouped, merge_up, preferred_element_type=jnp.float32), approximate=False
    ).astype(jnp.bfloat16)
    partial_sums = jnp.dot(merger_hidden, merge_down, preferred_element_type=jnp.float32)
    same_dest = dest[:, None] == dest[None, :]
    earlier = jnp.arange(img_dev)[:, None] > jnp.arange(img_dev)[None, :]
    slot_order = jnp.sum(same_dest & earlier, axis=1)
    send_place = dest * capacity + slot_order
    slot_buffer = jnp.full((seq_count * capacity,), tok_dev, jnp.int32).at[send_place].set(slot)
    slot_buffer = slot_buffer.reshape(seq_count, capacity)
    share_width = model_width // tp_count
    own_part = lax.axis_index("tp")
    merged = of_everyone(partial_sums, "tp").astype(jnp.bfloat16)
    buffer = jnp.zeros((seq_count * capacity, model_width), jnp.bfloat16).at[send_place].set(merged)
    buffer = buffer.reshape(seq_count, capacity, model_width)
    arrived, places = (
        lax.all_to_all(buffer, "seq", split_axis=0, concat_axis=0, tiled=True),
        lax.all_to_all(slot_buffer, "seq", split_axis=0, concat_axis=0, tiled=True),
    )
    layer_input = text.at[places.reshape(-1)].set(arrived.reshape(-1, model_width), mode="drop")
    layer_part = lax.dynamic_slice_in_dim(layer_input, own_part * share_width, share_width, 1)
    normed = rms_rows(layer_input).astype(jnp.bfloat16)
    pieces = sent_together((w_query, w_key, w_value), "seq", 0, 1)
    query_raw = jnp.dot(normed, pieces[0], preferred_element_type=jnp.float32)
    key_raw = jnp.dot(normed, pieces[1], preferred_element_type=jnp.float32)
    value_raw = jnp.dot(normed, pieces[2], preferred_element_type=jnp.float32)
    kv_local = w_key.shape[1] // HEAD
    group_size = w_query.shape[1] // w_key.shape[1]
    roped_query = rotate(query_raw.reshape(tok_dev, -1, HEAD), positions).astype(jnp.bfloat16)
    roped_query = roped_query.reshape(tok_dev, kv_local, group_size, HEAD)
    roped_key = rotate(key_raw.reshape(tok_dev, kv_local, HEAD), positions).astype(jnp.bfloat16)
    values = value_raw.reshape(tok_dev, kv_local, HEAD).astype(jnp.bfloat16)
    own_index = lax.axis_index("seq")
    queries = roped_query
    query_pos = own_index * tok_dev + jnp.arange(tok_dev, dtype=jnp.int32)
    last_query = jnp.max(query_pos)
    first_doc = jnp.min(documents)
    score_scale = HEAD ** (-0.5)

    def visit(carry, key_block, value_block, doc_block, key_first):
        unused = (key_first > last_query) | (doc_block[-1] < first_doc)
        return lax.cond(
            unused,
            lambda current: current,
            lambda current: attend(
                current,
                queries,
                key_block,
                value_block,
                doc_block,
                key_first,
                query_pos,
                documents,
                score_scale,
            ),
            carry,
        )

    initial = (
        jnp.full((kv_local, group_size, tok_dev), masked_score, jnp.float32),
        jnp.zeros((kv_local, group_size, tok_dev), jnp.float32),
        jnp.zeros((kv_local, group_size, tok_dev, HEAD), jnp.float32),
    )
    key_piece = lax.all_gather(roped_key, "seq", axis=0, tiled=True)
    value_piece = lax.all_gather(values, "seq", axis=0, tiled=True)
    doc_piece = lax.all_gather(documents, "seq", axis=0, tiled=True)
    piece_rows = key_piece.shape[0]
    block_count = piece_rows // block_rows
    stacked = (
        key_piece.reshape(block_count, block_rows, kv_local, HEAD),
        value_piece.reshape(block_count, block_rows, kv_local, HEAD),
        doc_piece.reshape(block_count, block_rows),
        jnp.arange(block_count, dtype=jnp.int32),
    )

    def through(current, parts):
        return (visit(current, parts[0], parts[1], parts[2], parts[3] * block_rows), None)

    finished, ignored = lax.scan(through, initial, stacked)
    maxima, totals, summed = finished
    attended = (
        (summed / totals[..., None]).transpose(2, 0, 1, 3).reshape(tok_dev, -1).astype(jnp.bfloat16)
    )
    return (layer_part, attended)


def solution(mesh):
    in_specs = (
        P("seq", None),
        P(None, "tp"),
        P("tp", None),
        P("seq"),
        P("seq"),
        P("seq", None),
        P(None, "seq"),
        P("seq"),
        P("seq", "tp"),
        P("seq", "tp"),
        P("seq", "tp"),
    )
    out_specs = (P("seq", "tp"), P("seq", "tp"))
    return jax.shard_map(
        per_device, mesh=mesh, in_specs=in_specs, out_specs=out_specs, check_vma=False
    )
```

profile of v0, /device:TPU:80, one launch (start us, length us, event | category | flops | bytes accessed | tf_op | source)
XLA Modules:
  0.0 469.6 jit_solution(3593981710146801849)
XLA Ops:
  9.7 12.3 %fusion.50 = f32[64,3584]{1,0:T(8,128)S(1)} fusion(bf16[1280,3584]{1,0:T(8,128)(2,1)} %param.17, bf16[64,5120]{1,0:T(8,128)(2,1)S(1)} %reshape.556, bf16[5120,1280]{1,0:T(8,128)(2,1)} %param.16), kind=kOutput, calls=%fused_computation.75 | convolution fusion | flops 1431388160 | bytes 23855104 | tf_op jit(solution)/shard_map/dot_general | solution.py:96
  23.4 3.7 all-to-all-start.1
  29.8 10.5 %all-to-all-start = ((s32[64,1,2]{2,1,0:T(1,128)}), s32[64,1,2]{2,1,0:T(1,128)S(1)}, u32[]{:S(2)}, u32[]{:S(2)}) async-start(s32[64,1,2]{2,1,0:T(1,128)} %bitcast.14), calls=%async_computation | async-start | bytes 65536 | tf_op jit(solution)/shard_map/all_to_all | solution.py:110
  46.4 9.1 %all-to-all-start.2 = ((bf16[64,2,3584]{2,1,0:T(2,128)(2,1)}), bf16[64,2,3584]{2,1,0:T(2,128)(2,1)S(1)}, u32[]{:S(2)}, u32[]{:S(2)}) async-start(bf16[64,2,3584]{2,1,0:T(2,128)(2,1)} %reshape.557), calls=%async_computation.2 | async-start | bytes 1835008 | tf_op jit(solution)/shard_map/all_to_all | solution.py:109
  56.8 11.5 %all-to-all-done.2 = bf16[64,2,3584]{2,1,0:T(2,128)(2,1)S(1)} async-done(((bf16[64,2,3584]{2,1,0:T(2,128)(2,1)}), bf16[64,2,3584]{2,1,0:T(2,128)(2,1)S(1)}, u32[]{:S(2)}, u32[]{:S(2)}) %all-to-all-start.2) | async-done | bytes 917536 | tf_op jit(solution)/shard_map/all_to_all | solution.py:109
  69.7 3.7 scatter_fusion
  73.8 16.7 %all-gather.6.cloned.1.call-done = bf16[3584,1152]{1,0:T(8,128)(2,1)} async-done(((bf16[56,1152]{1,0:T(8,128)(2,1)}), bf16[3584,1152]{1,0:T(8,128)(2,1)}) %all-gather.6.cloned.1.call-update) | async-done | bytes 8257552 | tf_op jit(solution)/shard_map/all_gather | solution.py:29
  93.6 2.5 convolution_convert_fusion
  97.5 138.7 %all-gather.1 = s32[64,1,256]{2,1,0:T(1,128)S(1)} all-gather(s32[1,1,256]{2,1,0:T(1,128)S(1)} %bitcast.97), channel_id=1, replica_groups=mesh['seq'=64,'tp'=2] {'seq'}, dimensions={0}, use_global_device_ids=true | all-gather | bytes 66560 | tf_op jit(solution)/shard_map/all_gather | solution.py:158
  237.7 5.5 %fusion.27 = f32[256,896]{0,1:T(8,128)S(1)} fusion(bf16[3584,1152]{1,0:T(8,128)(2,1)} %all-gather.6.cloned.1.call-done, bf16[256,3584]{1,0:T(8,128)(2,1)S(1)} %scatter_fusion, f32[256]{0:T(256)S(1)} %add_rsqrt_fusion), kind=kOutput, calls=%fused_computation.33 | convolution fusion | flops 1646919680 | bytes 9176064 | tf_op jit(solution)/shard_map/dot_general | solution.py:116
  243.7 6.4 %copy.44 = bf16[16384,1,128]{2,0,1:T(8,128)(2,1)} copy(bf16[16384,1,128]{0,2,1:T(8,128)(2,1)} %all-gather.8.cloned.1.call-done) | data formatting | bytes 8388608
  250.2 211.5 %while.15 = (s32[]{:T(128)}, f32[1,7,256]{2,1,0:T(8,128)S(1)}, f32[1,7,256]{2,1,0:T(8,128)S(1)}, f32[1,7,256,128]{3,2,1,0:T(8,128)S(1)}, s32[32]{0:T(128)S(1)}, ...) while((s32[]{:T(128)}, f32[1,7,256]{2,1,0:T(8,128)S(1)}, ...), condition=%wide.region_14.15_spmd.clone, body=%wide.region_9.14_spmd.clone.sunk | while | flops 482547712 | bytes 14221707 | solution.py:171
  269.5 5.2 %conditional.3 = (f32[1,7,256]{2,1,0:T(8,128)S(1)}, f32[1,7,256]{2,1,0:T(8,128)S(1)}, f32[1,7,256,128]{3,2,1,0:T(8,128)S(1)}) conditional(s32[]{:T(128)} %convert_element_type.127, (s32[]{:T(128)}, s32[]{:T(128)}, s32[256]{0:T(256)S(1)}, s32[1,512]{1,0:T(1,128)S(1)}, bf16[32,512,1,128]{3,1,2,0:T(8,128)(2,1)}, /*index=5*/s32[]{:T(128)}, ...), branch_computations={%region_10.12_spmd, %region_13.13_spmd} | conditional | flops 482547712 | bytes 14201888 | solution.py:134
  278.6 5.2 %conditional.3 = (f32[1,7,256]{2,1,0:T(8,128)S(1)}, f32[1,7,256]{2,1,0:T(8,128)S(1)}, f32[1,7,256,128]{3,2,1,0:T(8,128)S(1)}) conditional(s32[]{:T(128)} %convert_element_type.127, (s32[]{:T(128)}, s32[]{:T(128)}, s32[256]{0:T(256)S(1)}, s32[1,512]{1,0:T(1,128)S(1)}, bf16[32,512,1,128]{3,1,2,0:T(8,128)(2,1)}, /*index=5*/s32[]{:T(128)}, ...), branch_computations={%region_10.12_spmd, %region_13.13_spmd} | conditional | flops 482547712 | bytes 14201888 | solution.py:134
  287.6 5.2 %conditional.3 = (f32[1,7,256]{2,1,0:T(8,128)S(1)}, f32[1,7,256]{2,1,0:T(8,128)S(1)}, f32[1,7,256,128]{3,2,1,0:T(8,128)S(1)}) conditional(s32[]{:T(128)} %convert_element_type.127, (s32[]{:T(128)}, s32[]{:T(128)}, s32[256]{0:T(256)S(1)}, s32[1,512]{1,0:T(1,128)S(1)}, bf16[32,512,1,128]{3,1,2,0:T(8,128)(2,1)}, /*index=5*/s32[]{:T(128)}, ...), branch_computations={%region_10.12_spmd, %region_13.13_spmd} | conditional | flops 482547712 | bytes 14201888 | solution.py:134
  296.6 5.2 %conditional.3 = (f32[1,7,256]{2,1,0:T(8,128)S(1)}, f32[1,7,256]{2,1,0:T(8,128)S(1)}, f32[1,7,256,128]{3,2,1,0:T(8,128)S(1)}) conditional(s32[]{:T(128)} %convert_element_type.127, (s32[]{:T(128)}, s32[]{:T(128)}, s32[256]{0:T(256)S(1)}, s32[1,512]{1,0:T(1,128)S(1)}, bf16[32,512,1,128]{3,1,2,0:T(8,128)(2,1)}, /*index=5*/s32[]{:T(128)}, ...), branch_computations={%region_10.12_spmd, %region_13.13_spmd} | conditional | flops 482547712 | bytes 14201888 | solution.py:134
  298.5 2.3 fusion.12
  305.6 5.2 %conditional.3 = (f32[1,7,256]{2,1,0:T(8,128)S(1)}, f32[1,7,256]{2,1,0:T(8,128)S(1)}, f32[1,7,256,128]{3,2,1,0:T(8,128)S(1)}) conditional(s32[]{:T(128)} %convert_element_type.127, (s32[]{:T(128)}, s32[]{:T(128)}, s32[256]{0:T(256)S(1)}, s32[1,512]{1,0:T(1,128)S(1)}, bf16[32,512,1,128]{3,1,2,0:T(8,128)(2,1)}, /*index=5*/s32[]{:T(128)}, ...), branch_computations={%region_10.12_spmd, %region_13.13_spmd} | conditional | flops 482547712 | bytes 14201888 | solution.py:134
  314.6 5.2 %conditional.3 = (f32[1,7,256]{2,1,0:T(8,128)S(1)}, f32[1,7,256]{2,1,0:T(8,128)S(1)}, f32[1,7,256,128]{3,2,1,0:T(8,128)S(1)}) conditional(s32[]{:T(128)} %convert_element_type.127, (s32[]{:T(128)}, s32[]{:T(128)}, s32[256]{0:T(256)S(1)}, s32[1,512]{1,0:T(1,128)S(1)}, bf16[32,512,1,128]{3,1,2,0:T(8,128)(2,1)}, /*index=5*/s32[]{:T(128)}, ...), branch_computations={%region_10.12_spmd, %region_13.13_spmd} | conditional | flops 482547712 | bytes 14201888 | solution.py:134
  323.6 5.2 %conditional.3 = (f32[1,7,256]{2,1,0:T(8,128)S(1)}, f32[1,7,256]{2,1,0:T(8,128)S(1)}, f32[1,7,256,128]{3,2,1,0:T(8,128)S(1)}) conditional(s32[]{:T(128)} %convert_element_type.127, (s32[]{:T(128)}, s32[]{:T(128)}, s32[256]{0:T(256)S(1)}, s32[1,512]{1,0:T(1,128)S(1)}, bf16[32,512,1,128]{3,1,2,0:T(8,128)(2,1)}, /*index=5*/s32[]{:T(128)}, ...), branch_computations={%region_10.12_spmd, %region_13.13_spmd} | conditional | flops 482547712 | bytes 14201888 | solution.py:134
  332.6 5.2 %conditional.3 = (f32[1,7,256]{2,1,0:T(8,128)S(1)}, f32[1,7,256]{2,1,0:T(8,128)S(1)}, f32[1,7,256,128]{3,2,1,0:T(8,128)S(1)}) conditional(s32[]{:T(128)} %convert_element_type.127, (s32[]{:T(128)}, s32[]{:T(128)}, s32[256]{0:T(256)S(1)}, s32[1,512]{1,0:T(1,128)S(1)}, bf16[32,512,1,128]{3,1,2,0:T(8,128)(2,1)}, /*index=5*/s32[]{:T(128)}, ...), branch_computations={%region_10.12_spmd, %region_13.13_spmd} | conditional | flops 482547712 | bytes 14201888 | solution.py:134
  341.7 5.2 %conditional.3 = (f32[1,7,256]{2,1,0:T(8,128)S(1)}, f32[1,7,256]{2,1,0:T(8,128)S(1)}, f32[1,7,256,128]{3,2,1,0:T(8,128)S(1)}) conditional(s32[]{:T(128)} %convert_element_type.127, (s32[]{:T(128)}, s32[]{:T(128)}, s32[256]{0:T(256)S(1)}, s32[1,512]{1,0:T(1,128)S(1)}, bf16[32,512,1,128]{3,1,2,0:T(8,128)(2,1)}, /*index=5*/s32[]{:T(128)}, ...), branch_computations={%region_10.12_spmd, %region_13.13_spmd} | conditional | flops 482547712 | bytes 14201888 | solution.py:134
  350.7 5.2 %conditional.3 = (f32[1,7,256]{2,1,0:T(8,128)S(1)}, f32[1,7,256]{2,1,0:T(8,128)S(1)}, f32[1,7,256,128]{3,2,1,0:T(8,128)S(1)}) conditional(s32[]{:T(128)} %convert_element_type.127, (s32[]{:T(128)}, s32[]{:T(128)}, s32[256]{0:T(256)S(1)}, s32[1,512]{1,0:T(1,128)S(1)}, bf16[32,512,1,128]{3,1,2,0:T(8,128)(2,1)}, /*index=5*/s32[]{:T(128)}, ...), branch_computations={%region_10.12_spmd, %region_13.13_spmd} | conditional | flops 482547712 | bytes 14201888 | solution.py:134
  352.6 2.3 fusion.12
  359.7 5.2 %conditional.3 = (f32[1,7,256]{2,1,0:T(8,128)S(1)}, f32[1,7,256]{2,1,0:T(8,128)S(1)}, f32[1,7,256,128]{3,2,1,0:T(8,128)S(1)}) conditional(s32[]{:T(128)} %convert_element_type.127, (s32[]{:T(128)}, s32[]{:T(128)}, s32[256]{0:T(256)S(1)}, s32[1,512]{1,0:T(1,128)S(1)}, bf16[32,512,1,128]{3,1,2,0:T(8,128)(2,1)}, /*index=5*/s32[]{:T(128)}, ...), branch_computations={%region_10.12_spmd, %region_13.13_spmd} | conditional | flops 482547712 | bytes 14201888 | solution.py:134
  368.7 5.2 %conditional.3 = (f32[1,7,256]{2,1,0:T(8,128)S(1)}, f32[1,7,256]{2,1,0:T(8,128)S(1)}, f32[1,7,256,128]{3,2,1,0:T(8,128)S(1)}) conditional(s32[]{:T(128)} %convert_element_type.127, (s32[]{:T(128)}, s32[]{:T(128)}, s32[256]{0:T(256)S(1)}, s32[1,512]{1,0:T(1,128)S(1)}, bf16[32,512,1,128]{3,1,2,0:T(8,128)(2,1)}, /*index=5*/s32[]{:T(128)}, ...), branch_computations={%region_10.12_spmd, %region_13.13_spmd} | conditional | flops 482547712 | bytes 14201888 | solution.py:134
  377.7 5.2 %conditional.3 = (f32[1,7,256]{2,1,0:T(8,128)S(1)}, f32[1,7,256]{2,1,0:T(8,128)S(1)}, f32[1,7,256,128]{3,2,1,0:T(8,128)S(1)}) conditional(s32[]{:T(128)} %convert_element_type.127, (s32[]{:T(128)}, s32[]{:T(128)}, s32[256]{0:T(256)S(1)}, s32[1,512]{1,0:T(1,128)S(1)}, bf16[32,512,1,128]{3,1,2,0:T(8,128)(2,1)}, /*index=5*/s32[]{:T(128)}, ...), branch_computations={%region_10.12_spmd, %region_13.13_spmd} | conditional | flops 482547712 | bytes 14201888 | solution.py:134
  386.7 5.2 %conditional.3 = (f32[1,7,256]{2,1,0:T(8,128)S(1)}, f32[1,7,256]{2,1,0:T(8,128)S(1)}, f32[1,7,256,128]{3,2,1,0:T(8,128)S(1)}) conditional(s32[]{:T(128)} %convert_element_type.127, (s32[]{:T(128)}, s32[]{:T(128)}, s32[256]{0:T(256)S(1)}, s32[1,512]{1,0:T(1,128)S(1)}, bf16[32,512,1,128]{3,1,2,0:T(8,128)(2,1)}, /*index=5*/s32[]{:T(128)}, ...), branch_computations={%region_10.12_spmd, %region_13.13_spmd} | conditional | flops 482547712 | bytes 14201888 | solution.py:134
  395.7 5.2 %conditional.3 = (f32[1,7,256]{2,1,0:T(8,128)S(1)}, f32[1,7,256]{2,1,0:T(8,128)S(1)}, f32[1,7,256,128]{3,2,1,0:T(8,128)S(1)}) conditional(s32[]{:T(128)} %convert_element_type.127, (s32[]{:T(128)}, s32[]{:T(128)}, s32[256]{0:T(256)S(1)}, s32[1,512]{1,0:T(1,128)S(1)}, bf16[32,512,1,128]{3,1,2,0:T(8,128)(2,1)}, /*index=5*/s32[]{:T(128)}, ...), branch_computations={%region_10.12_spmd, %region_13.13_spmd} | conditional | flops 482547712 | bytes 14201888 | solution.py:134
  404.8 5.2 %conditional.3 = (f32[1,7,256]{2,1,0:T(8,128)S(1)}, f32[1,7,256]{2,1,0:T(8,128)S(1)}, f32[1,7,256,128]{3,2,1,0:T(8,128)S(1)}) conditional(s32[]{:T(128)} %convert_element_type.127, (s32[]{:T(128)}, s32[]{:T(128)}, s32[256]{0:T(256)S(1)}, s32[1,512]{1,0:T(1,128)S(1)}, bf16[32,512,1,128]{3,1,2,0:T(8,128)(2,1)}, /*index=5*/s32[]{:T(128)}, ...), branch_computations={%region_10.12_spmd, %region_13.13_spmd} | conditional | flops 482547712 | bytes 14201888 | solution.py:134
  406.7 2.3 fusion.12
  413.8 5.2 %conditional.3 = (f32[1,7,256]{2,1,0:T(8,128)S(1)}, f32[1,7,256]{2,1,0:T(8,128)S(1)}, f32[1,7,256,128]{3,2,1,0:T(8,128)S(1)}) conditional(s32[]{:T(128)} %convert_element_type.127, (s32[]{:T(128)}, s32[]{:T(128)}, s32[256]{0:T(256)S(1)}, s32[1,512]{1,0:T(1,128)S(1)}, bf16[32,512,1,128]{3,1,2,0:T(8,128)(2,1)}, /*index=5*/s32[]{:T(128)}, ...), branch_computations={%region_10.12_spmd, %region_13.13_spmd} | conditional | flops 482547712 | bytes 14201888 | solution.py:134
  (392 shorter events, 143.0 us)
Async XLA Ops:
  7.2 1.7 copy-start.1
  7.2 1.0 copy-start.2
  7.2 1.0 copy-start.5
  7.2 0.9 copy-start.4
  7.2 83.3 %all-gather.6.cloned.1.call-start = ((), (), s32[]{:S(2)}) async-start(), calls=%async_computation.3 | async-start | bytes 8386560 | tf_op jit(solution)/shard_map/all_gather | solution.py:29
  21.9 5.3 %copy-start.7 = (s32[64]{0:T(128)S(1)}, s32[64]{0:T(128)}, u32[]{:S(2)}) copy-start(s32[64]{0:T(128)} %param.18) | copy-start | bytes 772
  23.4 6.4 %all-to-all-start.1 = ((f32[2,64,3584]{2,1,0:T(8,128)}), f32[2,64,3584]{2,1,0:T(8,128)S(1)}, u32[]{:S(2)}, u32[]{:S(2)}) async-start(f32[2,64,3584]{2,1,0:T(8,128)} %broadcast_in_dim.137), calls=%async_computation.1 | async-start | bytes 3670016 | tf_op jit(solution)/shard_map/all_to_all | solution.py:15
  29.8 16.5 %all-to-all-start = ((s32[64,1,2]{2,1,0:T(1,128)}), s32[64,1,2]{2,1,0:T(1,128)S(1)}, u32[]{:S(2)}, u32[]{:S(2)}) async-start(s32[64,1,2]{2,1,0:T(1,128)} %bitcast.14), calls=%async_computation | async-start | bytes 65536 | tf_op jit(solution)/shard_map/all_to_all | solution.py:110
  40.4 15.1 %copy-start.6 = (s32[3,256]{1,0:T(4,128)S(1)}, s32[3,256]{1,0:T(4,128)}, u32[]{:S(2)}) copy-start(s32[3,256]{1,0:T(4,128)} %param.21) | copy-start | bytes 9220
  41.5 28.1 %copy-start = (bf16[256,3584]{1,0:T(8,128)(2,1)S(1)}, bf16[256,3584]{1,0:T(8,128)(2,1)}, u32[]{:S(2)}) copy-start(bf16[256,3584]{1,0:T(8,128)(2,1)} %param.20) | copy-start | bytes 5505028
  46.4 22.0 %all-to-all-start.2 = ((bf16[64,2,3584]{2,1,0:T(2,128)(2,1)}), bf16[64,2,3584]{2,1,0:T(2,128)(2,1)S(1)}, u32[]{:S(2)}, u32[]{:S(2)}) async-start(bf16[64,2,3584]{2,1,0:T(2,128)(2,1)} %reshape.557), calls=%async_computation.2 | async-start | bytes 1835008 | tf_op jit(solution)/shard_map/all_to_all | solution.py:109
  55.4 188.3 %all-gather.8.cloned.1.call-start = ((), (), s32[]{:S(2)}) async-start(), calls=%async_computation.4 | async-start | bytes 4259840 | tf_op jit(solution)/shard_map/all_gather | solution.py:156
  73.8 23.0 %copy-start.3 = (s32[256]{0:T(256)S(1)}, s32[256]{0:T(256)}, u32[]{:S(2)}) copy-start(s32[256]{0:T(256)} %param.22) | copy-start | bytes 3076
  93.5 156.6 %all-gather.10.cloned.1.call-start = ((), (), s32[]{:S(2)}) async-start(), calls=%async_computation.5 | async-start | bytes 4259840 | tf_op jit(solution)/shard_map/all_gather | solution.py:157
Sparse Core Ops, SparseCore 0:
  11.5 78.9 all-gather.5
  93.8 74.6 all-gather.7
  171.4 66.6 all-gather.9
where the time goes:
time: 472 us; the launch traced here: 470 us
  blocking collectives  139 us (29%)
  matrix products  89.6 us (19%)
  loops' own time  85.4 us (18%)
  local copies, waits for them, and re-layouts  60 us (13%)
  waiting for transfers between devices  30.4 us (6%)
  other arithmetic  28.1 us (6%)
  starting transfers between devices  23.4 us (5%)
  between operations  14.1 us (3%)
    all_gather x1, blocking collectives, per_device(): doc_piece = lax.all_gather(documents, 'seq', axis=0, tiled=True)  139 us
    another operation x1, loops' own time, per_device(): finished, ignored = lax.scan(through, initial, stacked)  83.7 us
    dot_general x17, matrix products, attend(): jnp.einsum('kgqp,pkd->kgqd', weights.astype(jnp.bfloat16), value_block, p...  39.7 us
    dot_general x17, matrix products, attend(): jnp.einsum('qkgd,pkd->kgqp', queries, key_block, preferred_element_type=j...  27.6 us
    dynamic_slice x64, local copies, waits for them, and re-layouts, per_device(): finished, ignored = lax.scan(through, initial, stacked)  20.2 us
    slice x32, local copies, waits for them, and re-layouts, visit(): unused = (key_first > last_query) | (doc_block[-1] < first_doc)  19.2 us
    all_gather x1, waiting for transfers between devices, sent_together(): lax.all_gather(both, axis, axis=dim, tiled=True)  16.7 us
    reduce_sum x17, other arithmetic, attend(): totals = totals * factor + jnp.sum(weights, axis=-1)  15.2 us
  transfers between devices with their start and end apart: 6, of which 4 were waited for; matrix products, arithmetic and copies ran while one was open for 10% of the time, Pallas kernels for 0%

commit v1 on v0

--- a/solution.py
+++ b/solution.py
@@ -8,6 +8,12 @@
 theta_base = 1000000.0
 masked_score = -1e30
 block_rows = 512
+
+
+def gather_from_all(x, axis, dim):
+    size = lax.axis_size(axis)
+    repeats = [size if d == dim else 1 for d in range(x.ndim)]
+    return lax.all_to_all(jnp.tile(x, repeats), axis, split_axis=dim, concat_axis=dim, tiled=True)
 
 
 def copy_for_each(x, axis):
@@ -155,7 +161,7 @@
     )
     key_piece = lax.all_gather(roped_key, "seq", axis=0, tiled=True)
     value_piece = lax.all_gather(values, "seq", axis=0, tiled=True)
-    doc_piece = lax.all_gather(documents, "seq", axis=0, tiled=True)
+    doc_piece = gather_from_all(documents, "seq", 0)
     piece_rows = key_piece.shape[0]
     block_count = piece_rows // block_rows
     stacked = (

time: 472 us -> 462 us (0.979)
  blocking collectives: 139 us -> 0 us
  waiting for transfers between devices: 30.4 us -> 147 us
  starting transfers between devices: 23.4 us -> 32.9 us
    all_gather x1 -> x0, blocking collectives: 139 us -> none  [per_device(): doc_piece = lax.all_gather(documents, 'seq', axis=0, tiled=True)]
    all_gather x1, waiting for transfers between devices: 0.01 us -> 63.2 us  [per_device(): value_piece = lax.all_gather(values, 'seq', axis=0, tiled=True)]
    all_gather x1, waiting for transfers between devices: 0.02 us -> 48.9 us  [per_device(): key_piece = lax.all_gather(roped_key, 'seq', axis=0, tiled=True)]
    all_to_all x0 -> x1, starting transfers between devices: none -> 9.46 us  [gather_from_all(): lax.all_to_all(jnp.tile(x, repeats), axis, split_axis=dim, concat_axis=di...]
  transfers between devices with their start and end apart: 6 -> 7, of which waited for: 4 -> 7; matrix products, arithmetic and copies ran while one was open for 10% -> 10% of each run, Pallas kernels for 0% -> 0%
where the time goes in v1:
time: 462 us; the launch traced here: 460 us
  waiting for transfers between devices  147 us (32%)
  matrix products  89.6 us (19%)
  loops' own time  85.1 us (18%)
  local copies, waits for them, and re-layouts  63 us (14%)
  starting transfers between devices  32.9 us (7%)
  other arithmetic  28.1 us (6%)
  between operations  14.1 us (3%)
    another operation x1, loops' own time, per_device(): finished, ignored = lax.scan(through, initial, stacked)  83.5 us
    all_gather x1, waiting for transfers between devices, per_device(): value_piece = lax.all_gather(values, 'seq', axis=0, tiled=True)  63.2 us
    all_gather x1, waiting for transfers between devices, per_device(): key_piece = lax.all_gather(roped_key, 'seq', axis=0, tiled=True)  48.9 us
    dot_general x17, matrix products, attend(): jnp.einsum('kgqp,pkd->kgqd', weights.astype(jnp.bfloat16), value_block, p...  39.7 us
    dot_general x17, matrix products, attend(): jnp.einsum('qkgd,pkd->kgqp', queries, key_block, preferred_element_type=j...  27.6 us
    dynamic_slice x64, local copies, waits for them, and re-layouts, per_device(): finished, ignored = lax.scan(through, initial, stacked)  21.8 us
    slice x32, local copies, waits for them, and re-layouts, visit(): unused = (key_first > last_query) | (doc_block[-1] < first_doc)  19.9 us
    all_gather x1, waiting for transfers between devices, sent_together(): lax.all_gather(both, axis, axis=dim, tiled=True)  16.7 us
  transfers between devices with their start and end apart: 7, of which 7 were waited for; matrix products, arithmetic and copies ran while one was open for 10% of the time, Pallas kernels for 0%

profile of v1, /device:TPU:80, one launch (start us, length us, event | category | flops | bytes accessed | tf_op | source)
XLA Modules:
  0.0 459.5 jit_solution(12012696142658947123)
XLA Ops:
  9.7 12.3 %fusion.50 = f32[64,3584]{1,0:T(8,128)S(1)} fusion(bf16[1280,3584]{1,0:T(8,128)(2,1)} %param.17, bf16[64,5120]{1,0:T(8,128)(2,1)S(1)} %reshape.561, bf16[5120,1280]{1,0:T(8,128)(2,1)} %param.16), kind=kOutput, calls=%fused_computation.75 | convolution fusion | flops 1431388160 | bytes 23855104 | tf_op jit(solution)/shard_map/dot_general | solution.py:102
  23.4 3.7 all-to-all-start.1
  29.8 10.5 %all-to-all-start = ((s32[64,1,2]{2,1,0:T(1,128)}), s32[64,1,2]{2,1,0:T(1,128)S(1)}, u32[]{:S(2)}, u32[]{:S(2)}) async-start(s32[64,1,2]{2,1,0:T(1,128)} %bitcast.14), calls=%async_computation | async-start | bytes 65536 | tf_op jit(solution)/shard_map/all_to_all | solution.py:116
  46.4 9.1 %all-to-all-start.2 = ((bf16[64,2,3584]{2,1,0:T(2,128)(2,1)}), bf16[64,2,3584]{2,1,0:T(2,128)(2,1)S(1)}, u32[]{:S(2)}, u32[]{:S(2)}) async-start(bf16[64,2,3584]{2,1,0:T(2,128)(2,1)} %reshape.562), calls=%async_computation.2 | async-start | bytes 1835008 | tf_op jit(solution)/shard_map/all_to_all | solution.py:115
  57.0 11.3 %all-to-all-done.2 = bf16[64,2,3584]{2,1,0:T(2,128)(2,1)S(1)} async-done(((bf16[64,2,3584]{2,1,0:T(2,128)(2,1)}), bf16[64,2,3584]{2,1,0:T(2,128)(2,1)S(1)}, u32[]{:S(2)}, u32[]{:S(2)}) %all-to-all-start.2) | async-done | bytes 917536 | tf_op jit(solution)/shard_map/all_to_all | solution.py:115
  69.7 3.7 scatter_fusion
  73.8 16.7 %all-gather.5.cloned.1.call-done = bf16[3584,1152]{1,0:T(8,128)(2,1)} async-done(((bf16[56,1152]{1,0:T(8,128)(2,1)}), bf16[3584,1152]{1,0:T(8,128)(2,1)}) %all-gather.5.cloned.1.call-update) | async-done | bytes 8257552 | tf_op jit(solution)/shard_map/all_gather | solution.py:35
  93.6 2.5 convolution_convert_fusion
  96.8 9.5 %all-to-all-start.3 = ((s32[64,256,1]{1,2,0:T(1,128)}), s32[64,256,1]{1,2,0:T(1,128)S(1)}, u32[]{:S(2)}, u32[]{:S(2)}) async-start(s32[64,256,1]{1,2,0:T(1,128)} %all_to_all.22), calls=%async_computation.3 | async-start | bytes 131072 | tf_op jit(solution)/shard_map/all_to_all | solution.py:16
  107.9 4.5 all-to-all-done.3
  113.5 5.5 %fusion.27 = f32[256,896]{0,1:T(8,128)S(1)} fusion(bf16[3584,1152]{1,0:T(8,128)(2,1)} %all-gather.5.cloned.1.call-done, bf16[256,3584]{1,0:T(8,128)(2,1)S(1)} %scatter_fusion, f32[256]{0:T(256)S(1)} %add_rsqrt_fusion), kind=kOutput, calls=%fused_computation.33 | convolution fusion | flops 1646919680 | bytes 9176064 | tf_op jit(solution)/shard_map/dot_general | solution.py:122
  119.5 48.9 %all-gather.7.cloned.1.call-done = bf16[16384,1,128]{0,2,1:T(8,128)(2,1)} async-done(((bf16[256,1,128]{0,2,1:T(8,128)(2,1)}), bf16[16384,1,128]{0,2,1:T(8,128)(2,1)}) %all-gather.7.cloned.1.call-update) | async-done | bytes 4194320 | tf_op jit(solution)/shard_map/all_gather | solution.py:162
  168.4 6.4 %copy.44 = bf16[16384,1,128]{2,0,1:T(8,128)(2,1)} copy(bf16[16384,1,128]{0,2,1:T(8,128)(2,1)} %all-gather.7.cloned.1.call-done) | data formatting | bytes 8388608
  174.7 63.2 %all-gather.9.cloned.1.call-done = bf16[16384,128]{1,0:T(8,128)(2,1)} async-done(((bf16[256,128]{1,0:T(8,128)(2,1)}), bf16[16384,128]{1,0:T(8,128)(2,1)}) %all-gather.9.cloned.1.call-update) | async-done | bytes 4194320 | tf_op jit(solution)/shard_map/all_gather | solution.py:163
  238.0 213.6 %while.15 = (s32[]{:T(128)}, f32[1,7,256]{2,1,0:T(8,128)S(1)}, f32[1,7,256]{2,1,0:T(8,128)S(1)}, f32[1,7,256,128]{3,2,1,0:T(8,128)S(1)}, s32[32]{0:T(128)S(1)}, ...) while((s32[]{:T(128)}, f32[1,7,256]{2,1,0:T(8,128)S(1)}, ...), condition=%wide.region_14.15_spmd.clone, body=%wide.region_9.14_spmd.clone.sunk | while | flops 482547712 | bytes 14221707 | solution.py:177
  257.7 5.2 %conditional.3 = (f32[1,7,256]{2,1,0:T(8,128)S(1)}, f32[1,7,256]{2,1,0:T(8,128)S(1)}, f32[1,7,256,128]{3,2,1,0:T(8,128)S(1)}) conditional(s32[]{:T(128)} %convert_element_type.127, (s32[]{:T(128)}, s32[]{:T(128)}, s32[256]{0:T(256)S(1)}, s32[1,512]{1,0:T(1,128)S(1)}, bf16[32,512,1,128]{3,1,2,0:T(8,128)(2,1)}, /*index=5*/s32[]{:T(128)}, ...), branch_computations={%region_10.12_spmd, %region_13.13_spmd} | conditional | flops 482547712 | bytes 14201888 | solution.py:140
  266.8 5.2 %conditional.3 = (f32[1,7,256]{2,1,0:T(8,128)S(1)}, f32[1,7,256]{2,1,0:T(8,128)S(1)}, f32[1,7,256,128]{3,2,1,0:T(8,128)S(1)}) conditional(s32[]{:T(128)} %convert_element_type.127, (s32[]{:T(128)}, s32[]{:T(128)}, s32[256]{0:T(256)S(1)}, s32[1,512]{1,0:T(1,128)S(1)}, bf16[32,512,1,128]{3,1,2,0:T(8,128)(2,1)}, /*index=5*/s32[]{:T(128)}, ...), branch_computations={%region_10.12_spmd, %region_13.13_spmd} | conditional | flops 482547712 | bytes 14201888 | solution.py:140
  275.9 5.2 %conditional.3 = (f32[1,7,256]{2,1,0:T(8,128)S(1)}, f32[1,7,256]{2,1,0:T(8,128)S(1)}, f32[1,7,256,128]{3,2,1,0:T(8,128)S(1)}) conditional(s32[]{:T(128)} %convert_element_type.127, (s32[]{:T(128)}, s32[]{:T(128)}, s32[256]{0:T(256)S(1)}, s32[1,512]{1,0:T(1,128)S(1)}, bf16[32,512,1,128]{3,1,2,0:T(8,128)(2,1)}, /*index=5*/s32[]{:T(128)}, ...), branch_computations={%region_10.12_spmd, %region_13.13_spmd} | conditional | flops 482547712 | bytes 14201888 | solution.py:140
  285.0 5.2 %conditional.3 = (f32[1,7,256]{2,1,0:T(8,128)S(1)}, f32[1,7,256]{2,1,0:T(8,128)S(1)}, f32[1,7,256,128]{3,2,1,0:T(8,128)S(1)}) conditional(s32[]{:T(128)} %convert_element_type.127, (s32[]{:T(128)}, s32[]{:T(128)}, s32[256]{0:T(256)S(1)}, s32[1,512]{1,0:T(1,128)S(1)}, bf16[32,512,1,128]{3,1,2,0:T(8,128)(2,1)}, /*index=5*/s32[]{:T(128)}, ...), branch_computations={%region_10.12_spmd, %region_13.13_spmd} | conditional | flops 482547712 | bytes 14201888 | solution.py:140
  294.0 5.2 %conditional.3 = (f32[1,7,256]{2,1,0:T(8,128)S(1)}, f32[1,7,256]{2,1,0:T(8,128)S(1)}, f32[1,7,256,128]{3,2,1,0:T(8,128)S(1)}) conditional(s32[]{:T(128)} %convert_element_type.127, (s32[]{:T(128)}, s32[]{:T(128)}, s32[256]{0:T(256)S(1)}, s32[1,512]{1,0:T(1,128)S(1)}, bf16[32,512,1,128]{3,1,2,0:T(8,128)(2,1)}, /*index=5*/s32[]{:T(128)}, ...), branch_computations={%region_10.12_spmd, %region_13.13_spmd} | conditional | flops 482547712 | bytes 14201888 | solution.py:140
  303.1 5.2 %conditional.3 = (f32[1,7,256]{2,1,0:T(8,128)S(1)}, f32[1,7,256]{2,1,0:T(8,128)S(1)}, f32[1,7,256,128]{3,2,1,0:T(8,128)S(1)}) conditional(s32[]{:T(128)} %convert_element_type.127, (s32[]{:T(128)}, s32[]{:T(128)}, s32[256]{0:T(256)S(1)}, s32[1,512]{1,0:T(1,128)S(1)}, bf16[32,512,1,128]{3,1,2,0:T(8,128)(2,1)}, /*index=5*/s32[]{:T(128)}, ...), branch_computations={%region_10.12_spmd, %region_13.13_spmd} | conditional | flops 482547712 | bytes 14201888 | solution.py:140
  312.2 5.2 %conditional.3 = (f32[1,7,256]{2,1,0:T(8,128)S(1)}, f32[1,7,256]{2,1,0:T(8,128)S(1)}, f32[1,7,256,128]{3,2,1,0:T(8,128)S(1)}) conditional(s32[]{:T(128)} %convert_element_type.127, (s32[]{:T(128)}, s32[]{:T(128)}, s32[256]{0:T(256)S(1)}, s32[1,512]{1,0:T(1,128)S(1)}, bf16[32,512,1,128]{3,1,2,0:T(8,128)(2,1)}, /*index=5*/s32[]{:T(128)}, ...), branch_computations={%region_10.12_spmd, %region_13.13_spmd} | conditional | flops 482547712 | bytes 14201888 | solution.py:140
  321.3 5.2 %conditional.3 = (f32[1,7,256]{2,1,0:T(8,128)S(1)}, f32[1,7,256]{2,1,0:T(8,128)S(1)}, f32[1,7,256,128]{3,2,1,0:T(8,128)S(1)}) conditional(s32[]{:T(128)} %convert_element_type.127, (s32[]{:T(128)}, s32[]{:T(128)}, s32[256]{0:T(256)S(1)}, s32[1,512]{1,0:T(1,128)S(1)}, bf16[32,512,1,128]{3,1,2,0:T(8,128)(2,1)}, /*index=5*/s32[]{:T(128)}, ...), branch_computations={%region_10.12_spmd, %region_13.13_spmd} | conditional | flops 482547712 | bytes 14201888 | solution.py:140
  330.4 5.2 %conditional.3 = (f32[1,7,256]{2,1,0:T(8,128)S(1)}, f32[1,7,256]{2,1,0:T(8,128)S(1)}, f32[1,7,256,128]{3,2,1,0:T(8,128)S(1)}) conditional(s32[]{:T(128)} %convert_element_type.127, (s32[]{:T(128)}, s32[]{:T(128)}, s32[256]{0:T(256)S(1)}, s32[1,512]{1,0:T(1,128)S(1)}, bf16[32,512,1,128]{3,1,2,0:T(8,128)(2,1)}, /*index=5*/s32[]{:T(128)}, ...), branch_computations={%region_10.12_spmd, %region_13.13_spmd} | conditional | flops 482547712 | bytes 14201888 | solution.py:140
  339.4 5.2 %conditional.3 = (f32[1,7,256]{2,1,0:T(8,128)S(1)}, f32[1,7,256]{2,1,0:T(8,128)S(1)}, f32[1,7,256,128]{3,2,1,0:T(8,128)S(1)}) conditional(s32[]{:T(128)} %convert_element_type.127, (s32[]{:T(128)}, s32[]{:T(128)}, s32[256]{0:T(256)S(1)}, s32[1,512]{1,0:T(1,128)S(1)}, bf16[32,512,1,128]{3,1,2,0:T(8,128)(2,1)}, /*index=5*/s32[]{:T(128)}, ...), branch_computations={%region_10.12_spmd, %region_13.13_spmd} | conditional | flops 482547712 | bytes 14201888 | solution.py:140
  348.5 5.2 %conditional.3 = (f32[1,7,256]{2,1,0:T(8,128)S(1)}, f32[1,7,256]{2,1,0:T(8,128)S(1)}, f32[1,7,256,128]{3,2,1,0:T(8,128)S(1)}) conditional(s32[]{:T(128)} %convert_element_type.127, (s32[]{:T(128)}, s32[]{:T(128)}, s32[256]{0:T(256)S(1)}, s32[1,512]{1,0:T(1,128)S(1)}, bf16[32,512,1,128]{3,1,2,0:T(8,128)(2,1)}, /*index=5*/s32[]{:T(128)}, ...), branch_computations={%region_10.12_spmd, %region_13.13_spmd} | conditional | flops 482547712 | bytes 14201888 | solution.py:140
  357.6 5.2 %conditional.3 = (f32[1,7,256]{2,1,0:T(8,128)S(1)}, f32[1,7,256]{2,1,0:T(8,128)S(1)}, f32[1,7,256,128]{3,2,1,0:T(8,128)S(1)}) conditional(s32[]{:T(128)} %convert_element_type.127, (s32[]{:T(128)}, s32[]{:T(128)}, s32[256]{0:T(256)S(1)}, s32[1,512]{1,0:T(1,128)S(1)}, bf16[32,512,1,128]{3,1,2,0:T(8,128)(2,1)}, /*index=5*/s32[]{:T(128)}, ...), branch_computations={%region_10.12_spmd, %region_13.13_spmd} | conditional | flops 482547712 | bytes 14201888 | solution.py:140
  366.7 5.2 %conditional.3 = (f32[1,7,256]{2,1,0:T(8,128)S(1)}, f32[1,7,256]{2,1,0:T(8,128)S(1)}, f32[1,7,256,128]{3,2,1,0:T(8,128)S(1)}) conditional(s32[]{:T(128)} %convert_element_type.127, (s32[]{:T(128)}, s32[]{:T(128)}, s32[256]{0:T(256)S(1)}, s32[1,512]{1,0:T(1,128)S(1)}, bf16[32,512,1,128]{3,1,2,0:T(8,128)(2,1)}, /*index=5*/s32[]{:T(128)}, ...), branch_computations={%region_10.12_spmd, %region_13.13_spmd} | conditional | flops 482547712 | bytes 14201888 | solution.py:140
  375.8 5.2 %conditional.3 = (f32[1,7,256]{2,1,0:T(8,128)S(1)}, f32[1,7,256]{2,1,0:T(8,128)S(1)}, f32[1,7,256,128]{3,2,1,0:T(8,128)S(1)}) conditional(s32[]{:T(128)} %convert_element_type.127, (s32[]{:T(128)}, s32[]{:T(128)}, s32[256]{0:T(256)S(1)}, s32[1,512]{1,0:T(1,128)S(1)}, bf16[32,512,1,128]{3,1,2,0:T(8,128)(2,1)}, /*index=5*/s32[]{:T(128)}, ...), branch_computations={%region_10.12_spmd, %region_13.13_spmd} | conditional | flops 482547712 | bytes 14201888 | solution.py:140
  384.8 5.2 %conditional.3 = (f32[1,7,256]{2,1,0:T(8,128)S(1)}, f32[1,7,256]{2,1,0:T(8,128)S(1)}, f32[1,7,256,128]{3,2,1,0:T(8,128)S(1)}) conditional(s32[]{:T(128)} %convert_element_type.127, (s32[]{:T(128)}, s32[]{:T(128)}, s32[256]{0:T(256)S(1)}, s32[1,512]{1,0:T(1,128)S(1)}, bf16[32,512,1,128]{3,1,2,0:T(8,128)(2,1)}, /*index=5*/s32[]{:T(128)}, ...), branch_computations={%region_10.12_spmd, %region_13.13_spmd} | conditional | flops 482547712 | bytes 14201888 | solution.py:140
  393.9 5.2 %conditional.3 = (f32[1,7,256]{2,1,0:T(8,128)S(1)}, f32[1,7,256]{2,1,0:T(8,128)S(1)}, f32[1,7,256,128]{3,2,1,0:T(8,128)S(1)}) conditional(s32[]{:T(128)} %convert_element_type.127, (s32[]{:T(128)}, s32[]{:T(128)}, s32[256]{0:T(256)S(1)}, s32[1,512]{1,0:T(1,128)S(1)}, bf16[32,512,1,128]{3,1,2,0:T(8,128)(2,1)}, /*index=5*/s32[]{:T(128)}, ...), branch_computations={%region_10.12_spmd, %region_13.13_spmd} | conditional | flops 482547712 | bytes 14201888 | solution.py:140
  403.0 5.2 %conditional.3 = (f32[1,7,256]{2,1,0:T(8,128)S(1)}, f32[1,7,256]{2,1,0:T(8,128)S(1)}, f32[1,7,256,128]{3,2,1,0:T(8,128)S(1)}) conditional(s32[]{:T(128)} %convert_element_type.127, (s32[]{:T(128)}, s32[]{:T(128)}, s32[256]{0:T(256)S(1)}, s32[1,512]{1,0:T(1,128)S(1)}, bf16[32,512,1,128]{3,1,2,0:T(8,128)(2,1)}, /*index=5*/s32[]{:T(128)}, ...), branch_computations={%region_10.12_spmd, %region_13.13_spmd} | conditional | flops 482547712 | bytes 14201888 | solution.py:140
  (394 shorter events, 153.1 us)
Async XLA Ops:
  7.2 1.7 copy-start.1
  7.2 1.0 copy-start.2
  7.2 1.0 copy-start.5
  7.2 0.9 copy-start.4
  7.2 83.3 %all-gather.5.cloned.1.call-start = ((), (), s32[]{:S(2)}) async-start(), calls=%async_computation.4 | async-start | bytes 8386560 | tf_op jit(solution)/shard_map/all_gather | solution.py:35
  21.9 5.2 %copy-start.7 = (s32[64]{0:T(128)S(1)}, s32[64]{0:T(128)}, u32[]{:S(2)}) copy-start(s32[64]{0:T(128)} %param.18) | copy-start | bytes 772
  23.4 6.4 %all-to-all-start.1 = ((f32[2,64,3584]{2,1,0:T(8,128)}), f32[2,64,3584]{2,1,0:T(8,128)S(1)}, u32[]{:S(2)}, u32[]{:S(2)}) async-start(f32[2,64,3584]{2,1,0:T(8,128)} %broadcast_in_dim.137), calls=%async_computation.1 | async-start | bytes 3670016 | tf_op jit(solution)/shard_map/all_to_all | solution.py:21
  29.8 16.5 %all-to-all-start = ((s32[64,1,2]{2,1,0:T(1,128)}), s32[64,1,2]{2,1,0:T(1,128)S(1)}, u32[]{:S(2)}, u32[]{:S(2)}) async-start(s32[64,1,2]{2,1,0:T(1,128)} %bitcast.14), calls=%async_computation | async-start | bytes 65536 | tf_op jit(solution)/shard_map/all_to_all | solution.py:116
  40.4 15.1 %copy-start.6 = (s32[3,256]{1,0:T(4,128)S(1)}, s32[3,256]{1,0:T(4,128)}, u32[]{:S(2)}) copy-start(s32[3,256]{1,0:T(4,128)} %param.21) | copy-start | bytes 9220
  41.5 28.1 %copy-start = (bf16[256,3584]{1,0:T(8,128)(2,1)S(1)}, bf16[256,3584]{1,0:T(8,128)(2,1)}, u32[]{:S(2)}) copy-start(bf16[256,3584]{1,0:T(8,128)(2,1)} %param.20) | copy-start | bytes 5505028
  46.4 22.0 %all-to-all-start.2 = ((bf16[64,2,3584]{2,1,0:T(2,128)(2,1)}), bf16[64,2,3584]{2,1,0:T(2,128)(2,1)S(1)}, u32[]{:S(2)}, u32[]{:S(2)}) async-start(bf16[64,2,3584]{2,1,0:T(2,128)(2,1)} %reshape.562), calls=%async_computation.2 | async-start | bytes 1835008 | tf_op jit(solution)/shard_map/all_to_all | solution.py:115
  55.4 112.9 %all-gather.7.cloned.1.call-start = ((), (), s32[]{:S(2)}) async-start(), calls=%async_computation.5 | async-start | bytes 4259840 | tf_op jit(solution)/shard_map/all_gather | solution.py:162
  73.8 22.3 %copy-start.3 = (s32[256]{0:T(256)S(1)}, s32[256]{0:T(256)}, u32[]{:S(2)}) copy-start(s32[256]{0:T(256)} %param.22) | copy-start | bytes 3076
  93.5 144.4 %all-gather.9.cloned.1.call-start = ((), (), s32[]{:S(2)}) async-start(), calls=%async_computation.6 | async-start | bytes 4259840 | tf_op jit(solution)/shard_map/all_gather | solution.py:163
  96.8 15.6 %all-to-all-start.3 = ((s32[64,256,1]{1,2,0:T(1,128)}), s32[64,256,1]{1,2,0:T(1,128)S(1)}, u32[]{:S(2)}, u32[]{:S(2)}) async-start(s32[64,256,1]{1,2,0:T(1,128)} %all_to_all.22), calls=%async_computation.3 | async-start | bytes 131072 | tf_op jit(solution)/shard_map/all_to_all | solution.py:16
Sparse Core Ops, SparseCore 0:
  11.5 78.9 all-gather.4
  93.7 74.6 all-gather.6
  171.3 66.6 all-gather.8
